TPU v7x, 32 devices: a whole 2x2x4 slice. The times are simulated.
32 devices in a mesh: lat: 8 (over z, y), lon: 4 (over x, core).
Axes of the slice: x: 2, y: 2, z: 4, core: 2. Of those that a mesh axis runs over, the one named last changes fastest.
Arguments:
- predicted_state: bfloat16 [222, 320, 512], P(None, 'lat', 'lon'), may hold values from -30 to 30
- observed_state: bfloat16 [222, 320, 512], P(None, 'lat', 'lon'), may hold values from -30 to 30
- longterm_average_state: bfloat16 [222, 320, 512], P(None, 'lat', 'lon'), may hold values from -30 to 30
Outputs:
- blurred_mismatch_map: bfloat16 [222, 320, 512], P(None, 'lat', 'lon')
- quadratic_mean_mistake: float32 [222], replicated
- pattern_agreement: float32 [222], replicated
All inputs are finite; a program needn't handle non-finite values.
Results may differ from a plain program's by a relative error of at most 0.00155.
Values may be sent and summed in bfloat16 or wider, within the bound.
A program may use at most 128 MiB of HBM per device.

v0:
```python
import jax
import jax.numpy as jnp
from jax import lax
from jax.sharding import PartitionSpec as P

epsilon = 1e-06


def extended(cells, sides, width):
    for axis, dim in sides:
        count = lax.axis_size(axis)
        head = lax.slice_in_dim(cells, 0, width, axis=dim)
        tail = lax.slice_in_dim(cells, cells.shape[dim] - width, cells.shape[dim], axis=dim)
        cells = jnp.concatenate(
            [
                lax.ppermute(tail, axis, [(i, (i + 1) % count) for i in range(count)]),
                cells,
                lax.ppermute(head, axis, [((i + 1) % count, i) for i in range(count)]),
            ],
            axis=dim,
        )
    return cells


def deviation_from_normal(predicted_state, observed_state, longterm_average_state):
    normal_reference_state = longterm_average_state.astype(jnp.float32)
    return (
        predicted_state.astype(jnp.float32) - normal_reference_state,
        observed_state.astype(jnp.float32) - normal_reference_state,
    )


def vertical_sum(member):
    return member[:, :-2] + member[:, 1:-1] + member[:, 2:]


def horizontal_sum(member):
    return member[:, :, :-2] + member[:, :, 1:-1] + member[:, :, 2:]


def finish(running_accumulations, grid_cells):
    mean_fcst = running_accumulations[1] / grid_cells
    mean_true = running_accumulations[2] / grid_cells
    variance_fcst = running_accumulations[3] / grid_cells - mean_fcst * mean_fcst
    variance_true = running_accumulations[4] / grid_cells - mean_true * mean_true
    covariance = running_accumulations[5] / grid_cells - mean_fcst * mean_true
    quadratic_mean_mistake = jnp.sqrt(running_accumulations[0] / grid_cells)
    pattern_agreement = covariance / jnp.sqrt((variance_fcst + epsilon) * (variance_true + epsilon))
    return (quadratic_mean_mistake, pattern_agreement)


def local(predicted_state, observed_state, longterm_average_state):
    nearby_parallel_accumulated = predicted_state.shape[1]
    parallel_overall_accumulated = nearby_parallel_accumulated * lax.axis_size("lat")
    meridian_accumulated = predicted_state.shape[2] * lax.axis_size("lon")
    row_start = lax.axis_index("lat") * nearby_parallel_accumulated
    row_index = row_start + jnp.arange(nearby_parallel_accumulated, dtype=jnp.int32)
    stacked_inputs = jnp.stack([predicted_state, observed_state, longterm_average_state])
    rimmed = extended(stacked_inputs, (("lat", 2), ("lon", 3)), 1)
    widened = deviation_from_normal(rimmed[0], rimmed[1], rimmed[2])
    padded_index = row_start - 1 + jnp.arange(nearby_parallel_accumulated + 2, dtype=jnp.int32)
    inside = ((padded_index >= 0) & (padded_index < parallel_overall_accumulated)).astype(
        jnp.float32
    )[None, :, None]
    summed = tuple((horizontal_sum(vertical_sum(member * inside)) for member in widened))
    row_count = (
        3.0
        - (row_index == 0).astype(jnp.float32)
        - (row_index == parallel_overall_accumulated - 1).astype(jnp.float32)
    )
    divisor = (3.0 * row_count)[:, None]
    averaged_prediction = summed[0] / divisor
    averaged_observation = summed[1] / divisor
    prediction_mismatch = averaged_prediction - averaged_observation
    all_rows = jnp.arange(parallel_overall_accumulated, dtype=jnp.float32)
    cosine = jnp.cos(jnp.pi * (0.5 - all_rows / (parallel_overall_accumulated - 1)))
    weight_all = cosine / jnp.mean(cosine)
    cosine_factor_vector = lax.dynamic_slice_in_dim(
        weight_all, row_start, nearby_parallel_accumulated
    )[:, None]
    weighted_fcst = cosine_factor_vector * averaged_prediction
    weighted_true = cosine_factor_vector * averaged_observation
    running_accumulations = jnp.stack(
        [
            jnp.sum(cosine_factor_vector * prediction_mismatch * prediction_mismatch, axis=(1, 2)),
            jnp.sum(weighted_fcst, axis=(1, 2)),
            jnp.sum(weighted_true, axis=(1, 2)),
            jnp.sum(weighted_fcst * averaged_prediction, axis=(1, 2)),
            jnp.sum(weighted_true * averaged_observation, axis=(1, 2)),
            jnp.sum(weighted_fcst * averaged_observation, axis=(1, 2)),
        ]
    )
    totals = lax.psum(running_accumulations, ("lat", "lon"))
    quadratic_mean_mistake, pattern_agreement = finish(
        totals, float(parallel_overall_accumulated * meridian_accumulated)
    )
    return (prediction_mismatch.astype(jnp.bfloat16), quadratic_mean_mistake, pattern_agreement)


def solution(mesh):
    placed = (P(None, "lat", "lon"), P(None, "lat", "lon"), P(None, "lat", "lon"))
    return jax.shard_map(
        local,
        mesh=mesh,
        in_specs=placed,
        out_specs=(P(None, "lat", "lon"), P(), P()),
        check_vma=False,
    )
```

profile of v0, /device:TPU:0, one launch (start us, length us, event | category | flops | bytes accessed | tf_op | source)
XLA Modules:
  0.0 139.8 jit_solution(17298895487577244605)
XLA Ops:
  0.6 4.5 %copy.6 = bf16[222,40,128]{0,1,2:T(8,128)(2,1)S(1)} copy(bf16[222,40,128]{2,1,0:T(8,128)(2,1)} %param.3) | data formatting | bytes 4546560 | tf_op args[0]
  5.1 5.2 %copy.7 = bf16[222,40,128]{0,1,2:T(8,128)(2,1)} copy(bf16[222,40,128]{2,1,0:T(8,128)(2,1)} %param.4) | data formatting | bytes 4546560 | tf_op args[1]
  10.3 5.3 %copy.8 = bf16[222,40,128]{0,1,2:T(8,128)(2,1)} copy(bf16[222,40,128]{2,1,0:T(8,128)(2,1)} %param.5) | data formatting | bytes 4546560 | tf_op args[2]
  15.6 3.1 %pad_maximum_fusion.3 = (bf16[3,222,1,128]{1,2,3,0:T(2,128)(2,1)}, bf16[3,222,1,128]{1,2,3,0:T(2,128)(2,1)}) fusion(bf16[1,222,40,128]{1,2,3,0:T(8,128)(2,1)} %bitcast.25, bf16[1,222,40,128]{1,2,3,0:T(8,128)(2,1)} %bitcast.22, bf16[1,222,40,128]{1,2,3,0:T(8,128)(2,1)S(1)} %bitcast.19), kind=kLoop, calls=%fused_computation.30 | loop fusion | flops 1022976 | bytes 7160832 | tf_op jit(solution)/shard_map/slice | solution.py:13
  18.7 3.0 %collective-permute-start = (bf16[3,222,1,128]{1,2,3,0:T(2,128)(2,1)}, bf16[3,222,1,128]{1,2,3,0:T(2,128)(2,1)S(1)}, u32[]{:S(2)}, u32[]{:S(2)}) collective-permute-start(bf16[3,222,1,128]{1,2,3,0:T(2,128)(2,1)} %get-tuple-element.18), channel_id=1, source_target_pairs={{0,4},{4,8},{8,12},{12,16},{16,20},{20,24},{24,28},{28,0},{1,5},{5... | collective-permute-start | bytes 511496 | tf_op jit(solution)/shard_map/ppermute | solution.py:16
  21.7 3.0 %collective-permute-start.1 = (bf16[3,222,1,128]{1,2,3,0:T(2,128)(2,1)}, bf16[3,222,1,128]{1,2,3,0:T(2,128)(2,1)S(1)}, u32[]{:S(2)}, u32[]{:S(2)}) collective-permute-start(bf16[3,222,1,128]{1,2,3,0:T(2,128)(2,1)} %get-tuple-element.19), channel_id=1, source_target_pairs={{4,0},{8,4},{12,8},{16,12},{20,16},{24,20},{28,24},{0,28},{5,1},{9... | collective-permute-start | bytes 511496 | tf_op jit(solution)/shard_map/ppermute | solution.py:18
  24.8 0.7 fusion.11
  26.1 0.5 fusion.19
  26.6 0.6 fusion.10
  27.2 11.6 %collective-permute-done = bf16[3,222,1,128]{1,2,3,0:T(2,128)(2,1)S(1)} collective-permute-done((bf16[3,222,1,128]{1,2,3,0:T(2,128)(2,1)}, bf16[3,222,1,128]{1,2,3,0:T(2,128)(2,1)S(1)}, u32[]{:S(2)}, u32[]{:S(2)}) %collective-permute-start) | collective-permute-done | bytes 170528 | tf_op jit(solution)/shard_map/ppermute | solution.py:16
  38.8 2.1 %collective-permute-done.1 = bf16[3,222,1,128]{1,2,3,0:T(2,128)(2,1)S(1)} collective-permute-done((bf16[3,222,1,128]{1,2,3,0:T(2,128)(2,1)}, bf16[3,222,1,128]{1,2,3,0:T(2,128)(2,1)S(1)}, u32[]{:S(2)}, u32[]{:S(2)}) %collective-permute-start.1) | collective-permute-done | bytes 170528 | tf_op jit(solution)/shard_map/ppermute | solution.py:18
  40.9 1.5 %pad_maximum_fusion.8 = (bf16[3,222,42,1]{1,2,3,0:T(8,128)(2,1)}, bf16[3,222,42,1]{1,2,3,0:T(8,128)(2,1)}) fusion(bf16[3,222,1,128]{1,2,3,0:T(2,128)(2,1)S(1)} %collective-permute-done.1, bf16[3,222,1,128]{1,2,3,0:T(2,128)(2,1)S(1)} %collective-permute-done, bf16[1,222,40,128]{1,2,3,0:T(8,128)(2,1)} %bitcast.26, bf16[1,222,40,128]{1,2,3,0:T(8,128)(2,1)} %bitcast.23, ...), kind=kLoop, calls=%fused_computation.35 | loop fusion | flops 559440 | bytes 7272720 | tf_op jit(solution)/shard_map/slice | solution.py:13
  42.4 0.0 collective-permute-start.2
  42.4 1.7 %collective-permute-start.3 = (bf16[3,222,42,1]{1,2,3,0:T(8,128)(2,1)}, bf16[3,222,42,1]{1,2,3,0:T(8,128)(2,1)S(1)}, u32[]{:S(2)}, u32[]{:S(2)}) collective-permute-start(bf16[3,222,42,1]{1,2,3,0:T(8,128)(2,1)} %get-tuple-element.17), channel_id=1, source_target_pairs={{1,0},{2,1},{3,2},{0,3},{5,4},{6,5},{7,6},{4,7},{9,8},{10,9},{11,1... | collective-permute-start | bytes 167840 | tf_op jit(solution)/shard_map/ppermute | solution.py:18
  44.2 0.5 and_convert_fusion
  44.7 0.7 dynamic_slice.3
  45.4 0.0 copy-start.1
  45.4 1.0 collective-permute-done.2
  46.4 0.1 collective-permute-done.3
  46.5 10.1 %pad_maximum_fusion = bf16[3,222,42,130]{1,2,3,0:T(8,128)(2,1)S(1)} fusion(bf16[3,222,42,1]{1,2,3,0:T(8,128)(2,1)S(1)} %collective-permute-done.3, bf16[3,222,1,128]{1,2,3,0:T(2,128)(2,1)S(1)} %collective-permute-done.1, bf16[1,222,40,128]{1,2,3,0:T(8,128)(2,1)} %bitcast.27, bf16[1,222,40,128]{1,2,3,0:T(8,128)(2,1)} %bitcast.24, ...), kind=kLoop, calls=%fused_computation | loop fusion | flops 50909040 | bytes 14545440 | tf_op jit(solution)/shard_map/concatenate | solution.py:14
  56.6 0.0 copy-done.1
  56.6 5.5 %fusion.1 = (f32[222,42,130]{0,1,2:T(8,128)}, f32[222,42,130]{0,1,2:T(8,128)}) fusion(bf16[3,222,42,130]{1,2,3,0:T(8,128)(2,1)S(1)} %pad_maximum_fusion, f32[42]{0:T(128)S(1)} %copy-done.1), kind=kLoop, calls=%fused_computation.10 | loop fusion | flops 8484840 | bytes 16969848 | tf_op jit(solution)/shard_map/mul | solution.py:65
  62.1 0.0 copy-start
  62.1 16.3 %slice_add_fusion = (f32[222,40,130]{0,1,2:T(8,128)S(1)}, f32[222,40,130]{0,1,2:T(8,128)}) fusion(f32[222,42,130]{0,1,2:T(8,128)} %get-tuple-element.15, f32[222,42,130]{0,1,2:T(8,128)} %get-tuple-element.14), kind=kLoop, calls=%fused_computation.13 | loop fusion | flops 4617600 | bytes 36940800 | tf_op jit(solution)/shard_map/add | solution.py:34
  78.4 0.0 copy-done
  78.4 12.7 %fusion.5 = (f32[222]{0:T(256)S(1)}, f32[222]{0:T(256)S(1)}, f32[222]{0:T(256)S(1)}, f32[222]{0:T(256)S(1)}, f32[222]{0:T(256)S(1)}, /*index=5*/f32[222]{0:T(256...) fusion(f32[40]{0:T(128)S(1)} %dynamic_slice.3, f32[40]{0:T(128)S(1)} %copy-done, f32[222,40,130]{0,1,2:T(8,128)S(1)} %get-tuple-element.22, ...), kind=kLoop, calls=%fused_computation.18 | loop fusion | flops 22731468 | bytes 36378128 | tf_op jit(solution)/shard_map/reduce_sum | solution.py:90
  91.1 39.4 %psum.7 = f32[6,222]{1,0:T(8,128)S(1)} all-reduce(f32[6,222]{1,0:T(8,128)S(1)} %stack.43), channel_id=1, replica_groups=mesh['lat'=8,'lon'=4] {'lat','lon'}, use_global_device_ids=true, to_apply=%region_7.0 | all-reduce | flops 1332 | bytes 10656 | tf_op jit(solution)/shard_map/psum | solution.py:93
  130.5 0.6 fusion.15
  131.1 4.9 %subtract_convert_fusion = bf16[222,40,128]{0,1,2:T(8,128)(2,1)S(1)} fusion(f32[222,40,128]{0,1,2:T(8,128)} %get-tuple-element.13, f32[222,40,128]{0,1,2:T(8,128)} %get-tuple-element.12), kind=kLoop, calls=%fused_computation.27 | loop fusion | flops 2273280 | bytes 11366400 | tf_op jit(solution)/shard_map/convert_element_type | solution.py:97
  136.0 3.8 %copy.9 = bf16[222,40,128]{2,1,0:T(8,128)(2,1)} copy(bf16[222,40,128]{0,1,2:T(8,128)(2,1)S(1)} %subtract_convert_fusion) | data formatting | bytes 4546560
  (1 shorter events, 0.0 us)
Async XLA Ops:
  18.7 20.1 %collective-permute-start = (bf16[3,222,1,128]{1,2,3,0:T(2,128)(2,1)}, bf16[3,222,1,128]{1,2,3,0:T(2,128)(2,1)S(1)}, u32[]{:S(2)}, u32[]{:S(2)}) collective-permute-start(bf16[3,222,1,128]{1,2,3,0:T(2,128)(2,1)} %get-tuple-element.18), channel_id=1, source_target_pairs={{0,4},{4,8},{8,12},{12,16},{16,20},{20,24},{24,28},{28,0},{1,5},{5... | collective-permute-start | bytes 511496 | tf_op jit(solution)/shard_map/ppermute | solution.py:16
  21.7 19.2 %collective-permute-start.1 = (bf16[3,222,1,128]{1,2,3,0:T(2,128)(2,1)}, bf16[3,222,1,128]{1,2,3,0:T(2,128)(2,1)S(1)}, u32[]{:S(2)}, u32[]{:S(2)}) collective-permute-start(bf16[3,222,1,128]{1,2,3,0:T(2,128)(2,1)} %get-tuple-element.19), channel_id=1, source_target_pairs={{4,0},{8,4},{12,8},{16,12},{20,16},{24,20},{28,24},{0,28},{5,1},{9... | collective-permute-start | bytes 511496 | tf_op jit(solution)/shard_map/ppermute | solution.py:18
  42.4 4.0 %collective-permute-start.2 = (bf16[3,222,42,1]{1,2,3,0:T(8,128)(2,1)}, bf16[3,222,42,1]{1,2,3,0:T(8,128)(2,1)S(1)}, u32[]{:S(2)}, u32[]{:S(2)}) collective-permute-start(bf16[3,222,42,1]{1,2,3,0:T(8,128)(2,1)} %get-tuple-element.16), channel_id=1, source_target_pairs={{0,1},{1,2},{2,3},{3,0},{4,5},{5,6},{6,7},{7,4},{8,9},{9,10},{10,1... | collective-permute-start | bytes 167840 | tf_op jit(solution)/shard_map/ppermute | solution.py:16
  42.4 4.0 %collective-permute-start.3 = (bf16[3,222,42,1]{1,2,3,0:T(8,128)(2,1)}, bf16[3,222,42,1]{1,2,3,0:T(8,128)(2,1)S(1)}, u32[]{:S(2)}, u32[]{:S(2)}) collective-permute-start(bf16[3,222,42,1]{1,2,3,0:T(8,128)(2,1)} %get-tuple-element.17), channel_id=1, source_target_pairs={{1,0},{2,1},{3,2},{0,3},{5,4},{6,5},{7,6},{4,7},{9,8},{10,9},{11,1... | collective-permute-start | bytes 167840 | tf_op jit(solution)/shard_map/ppermute | solution.py:18
  45.4 11.1 %copy-start.1 = (f32[42]{0:T(128)S(1)}, f32[42]{0:T(128)}, u32[]{:S(2)}) copy-start(f32[42]{0:T(128)} %and_convert_fusion) | copy-start | bytes 508
  62.1 16.3 %copy-start = (f32[40]{0:T(128)S(1)}, f32[40]{0:T(128)}, u32[]{:S(2)}) copy-start(f32[40]{0:T(128)} %fusion.19) | copy-start | bytes 484
where the time goes:
time: 140 us
  other arithmetic  57 us (41%)
  blocking collectives  39.4 us (28%)
  local copies, waits for them, and re-layouts  19.5 us (14%)
  waiting for transfers between devices  14.7 us (10%)
  starting transfers between devices  7.78 us (6%)
    psum x1, blocking collectives, local(): totals = lax.psum(running_accumulations, ('lat', 'lon'))  39.4 us
    unnamed x8, local copies, waits for them, and re-layouts  18.7 us
    add x1, other arithmetic, vertical_sum(): return member[:, :-2] + member[:, 1:-1] + member[:, 2:]  16.3 us
    reduce_sum x1, other arithmetic, local(): jnp.sum(weighted_fcst * averaged_observation, axis=(1, 2))  12.7 us
    ppermute x2, waiting for transfers between devices, extended(): lax.ppermute(tail, axis, [(i, (i + 1) % count) for i in range(count)])  12.6 us
    concatenate x1, other arithmetic, extended(): jnp.concatenate([lax.ppermute(tail, axis, [(i, (i + 1) % count) for i in...  10.1 us
    mul x1, other arithmetic, local(): member * inside  5.51 us
    convert_element_type x1, other arithmetic, local(): prediction_mismatch.astype(jnp.bfloat16)  4.93 us
  transfers between devices with their start and end apart: 4, of which 4 were waited for; matrix products, arithmetic and copies ran while one was open for 2% of the time, Pallas kernels for 0%

commit v1 on v0

--- a/solution.py
+++ b/solution.py
@@ -90,7 +90,9 @@
             jnp.sum(weighted_fcst * averaged_observation, axis=(1, 2)),
         ]
     )
-    totals = lax.psum(running_accumulations, ("lat", "lon"))
+    totals = running_accumulations
+    for num in ("lon", "lat"):
+        totals = lax.psum(totals, num)
     quadratic_mean_mistake, pattern_agreement = finish(
         totals, float(parallel_overall_accumulated * meridian_accumulated)
     )

time: 140 us -> 129 us (0.921)
  blocking collectives: 39.4 us -> 28.1 us
    psum x1 -> x2, blocking collectives: 39.4 us -> 28.1 us  [local(): totals = lax.psum(totals, num)]
where the time goes in v1:
time: 129 us
  other arithmetic  57 us (44%)
  blocking collectives  28.1 us (22%)
  local copies, waits for them, and re-layouts  19.5 us (15%)
  waiting for transfers between devices  14.7 us (11%)
  starting transfers between devices  7.78 us (6%)
  between operations  1.34 us (1%)
    psum x2, blocking collectives, local(): totals = lax.psum(totals, num)  28.1 us
    unnamed x8, local copies, waits for them, and re-layouts  18.7 us
    add x1, other arithmetic, vertical_sum(): return member[:, :-2] + member[:, 1:-1] + member[:, 2:]  16.3 us
    reduce_sum x1, other arithmetic, local(): jnp.sum(weighted_fcst * averaged_observation, axis=(1, 2))  12.7 us
    ppermute x2, waiting for transfers between devices, extended(): lax.ppermute(tail, axis, [(i, (i + 1) % count) for i in range(count)])  12.6 us
    concatenate x1, other arithmetic, extended(): jnp.concatenate([lax.ppermute(tail, axis, [(i, (i + 1) % count) for i in...  10.1 us
    mul x1, other arithmetic, local(): member * inside  5.51 us
    convert_element_type x1, other arithmetic, local(): prediction_mismatch.astype(jnp.bfloat16)  4.93 us
  transfers between devices with their start and end apart: 4, of which 4 were waited for; matrix products, arithmetic and copies ran while one was open for 2% of the time, Pallas kernels for 0%

profile of v1, /device:TPU:0, one launch (start us, length us, event | category | flops | bytes accessed | tf_op | source)
XLA Modules:
  0.0 128.5 jit_solution(118370961449659986)
XLA Ops:
  0.6 4.5 %copy.6 = bf16[222,40,128]{0,1,2:T(8,128)(2,1)S(1)} copy(bf16[222,40,128]{2,1,0:T(8,128)(2,1)} %param.3) | data formatting | bytes 4546560 | tf_op args[0]
  5.1 5.2 %copy.7 = bf16[222,40,128]{0,1,2:T(8,128)(2,1)} copy(bf16[222,40,128]{2,1,0:T(8,128)(2,1)} %param.4) | data formatting | bytes 4546560 | tf_op args[1]
  10.3 5.3 %copy.8 = bf16[222,40,128]{0,1,2:T(8,128)(2,1)} copy(bf16[222,40,128]{2,1,0:T(8,128)(2,1)} %param.5) | data formatting | bytes 4546560 | tf_op args[2]
  15.6 3.1 %pad_maximum_fusion.3 = (bf16[3,222,1,128]{1,2,3,0:T(2,128)(2,1)}, bf16[3,222,1,128]{1,2,3,0:T(2,128)(2,1)}) fusion(bf16[1,222,40,128]{1,2,3,0:T(8,128)(2,1)} %bitcast.25, bf16[1,222,40,128]{1,2,3,0:T(8,128)(2,1)} %bitcast.22, bf16[1,222,40,128]{1,2,3,0:T(8,128)(2,1)S(1)} %bitcast.19), kind=kLoop, calls=%fused_computation.30 | loop fusion | flops 1022976 | bytes 7160832 | tf_op jit(solution)/shard_map/slice | solution.py:13
  18.7 3.0 %collective-permute-start = (bf16[3,222,1,128]{1,2,3,0:T(2,128)(2,1)}, bf16[3,222,1,128]{1,2,3,0:T(2,128)(2,1)S(1)}, u32[]{:S(2)}, u32[]{:S(2)}) collective-permute-start(bf16[3,222,1,128]{1,2,3,0:T(2,128)(2,1)} %get-tuple-element.18), channel_id=1, source_target_pairs={{0,4},{4,8},{8,12},{12,16},{16,20},{20,24},{24,28},{28,0},{1,5},{5... | collective-permute-start | bytes 511496 | tf_op jit(solution)/shard_map/ppermute | solution.py:16
  21.7 3.0 %collective-permute-start.1 = (bf16[3,222,1,128]{1,2,3,0:T(2,128)(2,1)}, bf16[3,222,1,128]{1,2,3,0:T(2,128)(2,1)S(1)}, u32[]{:S(2)}, u32[]{:S(2)}) collective-permute-start(bf16[3,222,1,128]{1,2,3,0:T(2,128)(2,1)} %get-tuple-element.19), channel_id=1, source_target_pairs={{4,0},{8,4},{12,8},{16,12},{20,16},{24,20},{28,24},{0,28},{5,1},{9... | collective-permute-start | bytes 511496 | tf_op jit(solution)/shard_map/ppermute | solution.py:18
  24.8 0.7 fusion.11
  26.1 0.5 fusion.19
  26.6 0.6 fusion.10
  27.2 11.6 %collective-permute-done = bf16[3,222,1,128]{1,2,3,0:T(2,128)(2,1)S(1)} collective-permute-done((bf16[3,222,1,128]{1,2,3,0:T(2,128)(2,1)}, bf16[3,222,1,128]{1,2,3,0:T(2,128)(2,1)S(1)}, u32[]{:S(2)}, u32[]{:S(2)}) %collective-permute-start) | collective-permute-done | bytes 170528 | tf_op jit(solution)/shard_map/ppermute | solution.py:16
  38.8 2.1 %collective-permute-done.1 = bf16[3,222,1,128]{1,2,3,0:T(2,128)(2,1)S(1)} collective-permute-done((bf16[3,222,1,128]{1,2,3,0:T(2,128)(2,1)}, bf16[3,222,1,128]{1,2,3,0:T(2,128)(2,1)S(1)}, u32[]{:S(2)}, u32[]{:S(2)}) %collective-permute-start.1) | collective-permute-done | bytes 170528 | tf_op jit(solution)/shard_map/ppermute | solution.py:18
  40.9 1.5 %pad_maximum_fusion.8 = (bf16[3,222,42,1]{1,2,3,0:T(8,128)(2,1)}, bf16[3,222,42,1]{1,2,3,0:T(8,128)(2,1)}) fusion(bf16[3,222,1,128]{1,2,3,0:T(2,128)(2,1)S(1)} %collective-permute-done.1, bf16[3,222,1,128]{1,2,3,0:T(2,128)(2,1)S(1)} %collective-permute-done, bf16[1,222,40,128]{1,2,3,0:T(8,128)(2,1)} %bitcast.26, bf16[1,222,40,128]{1,2,3,0:T(8,128)(2,1)} %bitcast.23, ...), kind=kLoop, calls=%fused_computation.35 | loop fusion | flops 559440 | bytes 7272720 | tf_op jit(solution)/shard_map/slice | solution.py:13
  42.4 0.0 collective-permute-start.2
  42.4 1.7 %collective-permute-start.3 = (bf16[3,222,42,1]{1,2,3,0:T(8,128)(2,1)}, bf16[3,222,42,1]{1,2,3,0:T(8,128)(2,1)S(1)}, u32[]{:S(2)}, u32[]{:S(2)}) collective-permute-start(bf16[3,222,42,1]{1,2,3,0:T(8,128)(2,1)} %get-tuple-element.17), channel_id=1, source_target_pairs={{1,0},{2,1},{3,2},{0,3},{5,4},{6,5},{7,6},{4,7},{9,8},{10,9},{11,1... | collective-permute-start | bytes 167840 | tf_op jit(solution)/shard_map/ppermute | solution.py:18
  44.2 0.5 and_convert_fusion
  44.7 0.7 dynamic_slice.3
  45.4 0.0 copy-start.1
  45.4 1.0 collective-permute-done.2
  46.4 0.1 collective-permute-done.3
  46.5 10.1 %pad_maximum_fusion = bf16[3,222,42,130]{1,2,3,0:T(8,128)(2,1)S(1)} fusion(bf16[3,222,42,1]{1,2,3,0:T(8,128)(2,1)S(1)} %collective-permute-done.3, bf16[3,222,1,128]{1,2,3,0:T(2,128)(2,1)S(1)} %collective-permute-done.1, bf16[1,222,40,128]{1,2,3,0:T(8,128)(2,1)} %bitcast.27, bf16[1,222,40,128]{1,2,3,0:T(8,128)(2,1)} %bitcast.24, ...), kind=kLoop, calls=%fused_computation | loop fusion | flops 50909040 | bytes 14545440 | tf_op jit(solution)/shard_map/concatenate | solution.py:14
  56.6 0.0 copy-done.1
  56.6 5.5 %fusion.1 = (f32[222,42,130]{0,1,2:T(8,128)}, f32[222,42,130]{0,1,2:T(8,128)}) fusion(bf16[3,222,42,130]{1,2,3,0:T(8,128)(2,1)S(1)} %pad_maximum_fusion, f32[42]{0:T(128)S(1)} %copy-done.1), kind=kLoop, calls=%fused_computation.10 | loop fusion | flops 8484840 | bytes 16969848 | tf_op jit(solution)/shard_map/mul | solution.py:65
  62.1 0.0 copy-start
  62.1 16.3 %slice_add_fusion = (f32[222,40,130]{0,1,2:T(8,128)S(1)}, f32[222,40,130]{0,1,2:T(8,128)}) fusion(f32[222,42,130]{0,1,2:T(8,128)} %get-tuple-element.15, f32[222,42,130]{0,1,2:T(8,128)} %get-tuple-element.14), kind=kLoop, calls=%fused_computation.13 | loop fusion | flops 4617600 | bytes 36940800 | tf_op jit(solution)/shard_map/add | solution.py:34
  78.4 0.0 copy-done
  78.4 12.7 %fusion.5 = (f32[222]{0:T(256)S(1)}, f32[222]{0:T(256)S(1)}, f32[222]{0:T(256)S(1)}, f32[222]{0:T(256)S(1)}, f32[222]{0:T(256)S(1)}, /*index=5*/f32[222]{0:T(256...) fusion(f32[40]{0:T(128)S(1)} %dynamic_slice.3, f32[40]{0:T(128)S(1)} %copy-done, f32[222,40,130]{0,1,2:T(8,128)S(1)} %get-tuple-element.22, ...), kind=kLoop, calls=%fused_computation.18 | loop fusion | flops 22731468 | bytes 36378128 | tf_op jit(solution)/shard_map/reduce_sum | solution.py:90
  91.1 7.4 %psum.14 = f32[6,222]{1,0:T(8,128)S(1)} all-reduce(f32[6,222]{1,0:T(8,128)S(1)} %stack.43), channel_id=1, replica_groups=mesh['lat'=8,'lon'=4] {'lon'}, use_global_device_ids=true, to_apply=%region_7.0 | all-reduce | flops 1332 | bytes 10656 | tf_op jit(solution)/shard_map/psum | solution.py:95
  98.5 20.7 %psum.15 = f32[6,222]{1,0:T(8,128)S(1)} all-reduce(f32[6,222]{1,0:T(8,128)S(1)} %psum.14), channel_id=1, replica_groups=mesh['lat'=8,'lon'=4] {'lat'}, use_global_device_ids=true, to_apply=%region_8.0 | all-reduce | flops 1332 | bytes 10656 | tf_op jit(solution)/shard_map/psum | solution.py:95
  119.2 0.6 fusion.15
  119.8 4.9 %subtract_convert_fusion = bf16[222,40,128]{0,1,2:T(8,128)(2,1)S(1)} fusion(f32[222,40,128]{0,1,2:T(8,128)} %get-tuple-element.13, f32[222,40,128]{0,1,2:T(8,128)} %get-tuple-element.12), kind=kLoop, calls=%fused_computation.27 | loop fusion | flops 2273280 | bytes 11366400 | tf_op jit(solution)/shard_map/convert_element_type | solution.py:99
  124.8 3.8 %copy.9 = bf16[222,40,128]{2,1,0:T(8,128)(2,1)} copy(bf16[222,40,128]{0,1,2:T(8,128)(2,1)S(1)} %subtract_convert_fusion) | data formatting | bytes 4546560
  (1 shorter events, 0.0 us)
Async XLA Ops:
  18.7 20.1 %collective-permute-start = (bf16[3,222,1,128]{1,2,3,0:T(2,128)(2,1)}, bf16[3,222,1,128]{1,2,3,0:T(2,128)(2,1)S(1)}, u32[]{:S(2)}, u32[]{:S(2)}) collective-permute-start(bf16[3,222,1,128]{1,2,3,0:T(2,128)(2,1)} %get-tuple-element.18), channel_id=1, source_target_pairs={{0,4},{4,8},{8,12},{12,16},{16,20},{20,24},{24,28},{28,0},{1,5},{5... | collective-permute-start | bytes 511496 | tf_op jit(solution)/shard_map/ppermute | solution.py:16
  21.7 19.2 %collective-permute-start.1 = (bf16[3,222,1,128]{1,2,3,0:T(2,128)(2,1)}, bf16[3,222,1,128]{1,2,3,0:T(2,128)(2,1)S(1)}, u32[]{:S(2)}, u32[]{:S(2)}) collective-permute-start(bf16[3,222,1,128]{1,2,3,0:T(2,128)(2,1)} %get-tuple-element.19), channel_id=1, source_target_pairs={{4,0},{8,4},{12,8},{16,12},{20,16},{24,20},{28,24},{0,28},{5,1},{9... | collective-permute-start | bytes 511496 | tf_op jit(solution)/shard_map/ppermute | solution.py:18
  42.4 4.0 %collective-permute-start.2 = (bf16[3,222,42,1]{1,2,3,0:T(8,128)(2,1)}, bf16[3,222,42,1]{1,2,3,0:T(8,128)(2,1)S(1)}, u32[]{:S(2)}, u32[]{:S(2)}) collective-permute-start(bf16[3,222,42,1]{1,2,3,0:T(8,128)(2,1)} %get-tuple-element.16), channel_id=1, source_target_pairs={{0,1},{1,2},{2,3},{3,0},{4,5},{5,6},{6,7},{7,4},{8,9},{9,10},{10,1... | collective-permute-start | bytes 167840 | tf_op jit(solution)/shard_map/ppermute | solution.py:16
  42.4 4.0 %collective-permute-start.3 = (bf16[3,222,42,1]{1,2,3,0:T(8,128)(2,1)}, bf16[3,222,42,1]{1,2,3,0:T(8,128)(2,1)S(1)}, u32[]{:S(2)}, u32[]{:S(2)}) collective-permute-start(bf16[3,222,42,1]{1,2,3,0:T(8,128)(2,1)} %get-tuple-element.17), channel_id=1, source_target_pairs={{1,0},{2,1},{3,2},{0,3},{5,4},{6,5},{7,6},{4,7},{9,8},{10,9},{11,1... | collective-permute-start | bytes 167840 | tf_op jit(solution)/shard_map/ppermute | solution.py:18
  45.4 11.1 %copy-start.1 = (f32[42]{0:T(128)S(1)}, f32[42]{0:T(128)}, u32[]{:S(2)}) copy-start(f32[42]{0:T(128)} %and_convert_fusion) | copy-start | bytes 508
  62.1 16.3 %copy-start = (f32[40]{0:T(128)S(1)}, f32[40]{0:T(128)}, u32[]{:S(2)}) copy-start(f32[40]{0:T(128)} %fusion.19) | copy-start | bytes 484
